TPU v7x, 32 devices: a whole 2x2x4 slice. The times are simulated.
32 devices in a mesh: band: 8 (over z, x), gvec: 4 (over y, core).
Axes of the slice: x: 2, y: 2, z: 4, core: 2. Of those that a mesh axis runs over, the one named last changes fastest.
Arguments:
- wave_coeffs: bfloat16 [2, 256, 75264], P(None, 'band', 'gvec'), may hold values from -6 to 6
- projectors: bfloat16 [2, 64, 75264], P(None, 'band', 'gvec'), may hold values from -0.0234375 to 0.0234375
- miller_index: int32 [3, 75264], P(None, 'gvec'), may hold values from -24 to 24
- lattice: float32 [3, 3], replicated, may hold values from -0.25 to 1.25
- occupation: float32 [256], P('band'), may hold values from 0 to 2
- species: int32 [8], replicated, may hold values from 0 to 3
- proj_count: int32 [8], replicated, may hold values from 4 to 8
- coupling: float32 [4, 8, 8], replicated, may hold values from -0.4 to 2, as said below
Outputs:
- forces: float32 [3, 8], P(None, 'band')
- stress: float32 [3, 3], replicated
Inputs may be any that keep to these rules, and one draw needn't show every extreme that they name: `coupling`: symmetric in its last two dimensions.
All inputs are finite; a program needn't handle non-finite values.
Results may differ from a plain program's by a relative error of at most 0.006.
Values may be sent and summed in bfloat16 or wider, within the bound.
A program may use at most 64 MiB of HBM per device.

v0:
```python
import math

import jax
import jax.numpy as jnp
from jax import lax
from jax.sharding import PartitionSpec as P

PROJ = 8
MILLER = 24


stress_pairs = ((0, 0), (1, 1), (2, 2), (0, 1), (0, 2), (1, 2))


def cart_weights(miller_index, lattice):
    indices = miller_index.astype(jnp.float32)
    coords = []
    for column in range(3):
        coords.append(
            (
                indices[0] * lattice[0, column]
                + indices[1] * lattice[1, column]
                + indices[2] * lattice[2, column]
            )
            / MILLER
        )
    isotropic = (coords[0] * coords[0] + coords[1] * coords[1] + coords[2] * coords[2]) / 3.0
    weight_rows = [jnp.ones_like(coords[0])] + coords
    for first_axis, second_axis in stress_pairs:
        product = coords[first_axis] * coords[second_axis]
        if first_axis == second_axis:
            product = product - isotropic
        weight_rows.append(product)
    return jnp.stack(weight_rows)


def scale_block(weights, atom_block):
    proj_rows = atom_block.shape[1]
    scaled = (weights[:, None, None, :] * atom_block[None].astype(jnp.float32)).astype(jnp.bfloat16)
    return scaled.reshape(20 * proj_rows, atom_block.shape[2])


def intersection(scaled, flat_waves):
    product = lax.dot_general(
        scaled, flat_waves, (((1,), (1,)), ((), ())), preferred_element_type=jnp.float32
    )
    product = product.reshape(10, 2, scaled.shape[0] // 20, 2, flat_waves.shape[0] // 2)
    real_part = product[:, 0, :, 0] + product[:, 1, :, 1]
    imag_part = product[:, 0, :, 1] - product[:, 1, :, 0]
    return jnp.stack([real_part, imag_part], axis=1)


def atom_couplings(species, proj_count, coupling):
    kind_count = coupling.shape[0]
    proj_width = coupling.shape[1]
    onehot = (species[:, None] == jnp.arange(kind_count, dtype=jnp.int32)[None, :]).astype(
        jnp.float32
    )
    chosen = jnp.einsum("as,sij->aij", onehot, coupling, precision=lax.Precision.HIGHEST)
    active = (jnp.arange(proj_width, dtype=jnp.int32)[None, :] < proj_count[:, None]).astype(
        jnp.float32
    )
    return chosen * active[:, :, None] * active[:, None, :]


def contract(per_atom, couplings, occupied):
    mixed = jnp.einsum("aij,kcajn->kcain", couplings, per_atom, precision=lax.Precision.HIGHEST)
    becp_real = per_atom[0, 0]
    becp_imag = per_atom[0, 1]
    imag_sum = jnp.sum(becp_real[None] * mixed[1:4, 1] - becp_imag[None] * mixed[1:4, 0], axis=2)
    real_sum = jnp.sum(becp_real[None] * mixed[4:, 0] + becp_imag[None] * mixed[4:, 1], axis=2)
    force_part = jnp.sum(imag_sum * occupied, axis=2)
    stress_part = jnp.sum(real_sum * occupied, axis=(1, 2))
    return (force_part, stress_part)


def stress_matrix(values):
    return jnp.stack(
        [
            jnp.stack([values[0], values[3], values[4]]),
            jnp.stack([values[3], values[1], values[5]]),
            jnp.stack([values[4], values[5], values[2]]),
        ]
    )


def body(wave_coeffs, projectors, miller_index, lattice, occupation, species, proj_count, coupling):
    weights = cart_weights(miller_index, lattice)
    band_count = wave_coeffs.shape[1]
    quarter_count = band_count // lax.axis_size("gvec")
    group_slot = lax.axis_index("gvec")
    atom_total = species.shape[0]
    flat_waves = wave_coeffs.reshape(2 * band_count, wave_coeffs.shape[2])
    total_proj = PROJ * lax.axis_size("band")
    start_carry = jnp.zeros((band_count, 10, 2, total_proj), jnp.float32)
    arrived = lax.all_gather(projectors, "band", axis=1, tiled=True)
    block_rows = arrived.shape[1]
    anchor = jnp.zeros((), jnp.int32)

    def one_atom(atom_slot, partial_value):
        atom_block = lax.dynamic_slice_in_dim(arrived, atom_slot * PROJ, PROJ, 1)
        values = intersection(scale_block(weights, atom_block), flat_waves).transpose(3, 0, 1, 2)
        return lax.dynamic_update_slice(
            partial_value, values, (anchor, anchor, anchor, atom_slot * PROJ)
        )

    intersections = lax.fori_loop(0, block_rows // PROJ, one_atom, start_carry)
    couplings = atom_couplings(species, proj_count, coupling)
    owned_rows = lax.psum_scatter(intersections, "gvec", scatter_dimension=0, tiled=True)
    occupied = lax.dynamic_slice_in_dim(occupation, group_slot * quarter_count, quarter_count, 0)
    per_atom = owned_rows.reshape(quarter_count, 10, 2, atom_total, PROJ).transpose(1, 2, 3, 4, 0)
    force_part, stress_part = contract(per_atom, couplings, occupied)
    band_total = band_count * lax.axis_size("band")
    force_scale = 2.0 / (PROJ * math.sqrt(band_total))
    stress_scale = 1.0 / (PROJ * math.sqrt(atom_total * band_total))
    all_force, total_stress = lax.psum((force_part, stress_part), ("band", "gvec"))
    owned_atoms = atom_total // lax.axis_size("band")
    own_force = lax.dynamic_slice_in_dim(
        all_force, lax.axis_index("band") * owned_atoms, owned_atoms, 1
    )
    return (own_force * force_scale, stress_matrix(total_stress * stress_scale))


def solution(mesh):
    return jax.shard_map(
        body,
        mesh=mesh,
        in_specs=(
            P(None, "band", "gvec"),
            P(None, "band", "gvec"),
            P(None, "gvec"),
            P(),
            P("band"),
            P(),
            P(),
            P(),
        ),
        out_specs=(P(None, "band"), P()),
        check_vma=False,
    )
```

profile of v0, /device:TPU:0, one launch (start us, length us, event | category | flops | bytes accessed | tf_op | source)
XLA Modules:
  0.0 217.9 jit_solution(4178742472580967056)
XLA Ops:
  7.2 0.7 all-gather.2.cloned.1.call-update
  8.0 1.7 fusion.27
  9.7 1.0 convert_element_type.32
  10.7 0.7 fusion.21
  11.4 0.1 copy.31
  11.5 1.2 dynamic-slice
  13.3 0.7 dynamic_slice.13
  14.1 4.2 %fusion.25 = (f32[1,18816]{1,0:T(1,128)S(1)}, f32[1,18816]{1,0:T(1,128)S(1)}, f32[1,18816]{1,0:T(1,128)S(1)}) fusion(f32[]{:T(128)} %bitcast.16, f32[3,18816]{1,0:T(4,128)S(1)} %convert_element_type.32, f32[]{:T(128)} %bitcast.15, f32[]{:T(128)} %bitcast.14, f32[]{:T(128)} %bitcast.13, f32[]{:T(128)} %bitcast.12, f32[]{:T(128)} %bitcast.11), kind=kLoop, calls=%fused_computation.55 | loop fusion | flops 244608 | bytes 451608 | tf_op jit(solution)/shard_map/mul | solution.py:30
  18.3 2.1 fusion.26
  20.4 0.2 multiply_subtract_fusion
  20.6 0.1 multiply_subtract_fusion.1
  20.8 1.3 stack.48
  22.0 71.5 %all-gather.2.cloned.1.call-done = bf16[2,64,18816]{2,1,0:T(8,128)(2,1)} async-done(((bf16[2,8,18816]{2,1,0:T(8,128)(2,1)}), bf16[2,64,18816]{2,1,0:T(8,128)(2,1)}) %all-gather.2.cloned.1.call-update) | async-done | bytes 4816912 | tf_op jit(solution)/shard_map/all_gather | solution.py:96
  93.6 37.3 %while.13 = (s32[]{:T(128)}, f32[32,10,2,64]{0,3,1,2:T(8,128)S(1)}, f32[10,18816]{1,0:T(8,128)S(1)}, bf16[2,64,18816]{2,1,0:T(8,128)(2,1)}, bf16[64,18816]{1,0:T...) while((s32[]{:T(128)}, f32[32,10,2,64]{0,3,1,2:T(8,128)S(1)}, f32[10,18816]{1,0:T(8,128)S(1)}, ...), condition=%wide.region_1.0_spmd, body=%wide.region_0.0_spmd.sunk | while | flops 391684096 | bytes 6438035 | solution.py:107
  93.6 1.2 dynamic-slice_convert_fusion.2
  94.8 3.4 %fusion.40 = f32[10,2,8,2,32]{4,2,3,1,0:T(8,128)S(1)} fusion(bf16[2,32,18816,1,1]{2,1,0,4,3:T(8,128)(2,1)} %bitcast.110, f32[2,8,18816]{2,1,0:T(8,128)S(1)} %dynamic-slice_convert_fusion.2, f32[10,18816]{1,0:T(8,128)S(1)} %get-tuple-element.190), kind=kOutput, calls=%fused_computation.2.clone.1 | convolution fusion | flops 391372800 | bytes 4406272 | tf_op jit(solution)/shard_map/while/body/eval_jaxpr/dot_general | solution.py:44
  98.3 1.2 dynamic-slice_convert_fusion.2
  99.4 3.4 %fusion.40 = f32[10,2,8,2,32]{4,2,3,1,0:T(8,128)S(1)} fusion(bf16[2,32,18816,1,1]{2,1,0,4,3:T(8,128)(2,1)} %bitcast.110, f32[2,8,18816]{2,1,0:T(8,128)S(1)} %dynamic-slice_convert_fusion.2, f32[10,18816]{1,0:T(8,128)S(1)} %get-tuple-element.190), kind=kOutput, calls=%fused_computation.2.clone.1 | convolution fusion | flops 391372800 | bytes 4406272 | tf_op jit(solution)/shard_map/while/body/eval_jaxpr/dot_general | solution.py:44
  102.9 1.2 dynamic-slice_convert_fusion.2
  104.1 3.4 %fusion.40 = f32[10,2,8,2,32]{4,2,3,1,0:T(8,128)S(1)} fusion(bf16[2,32,18816,1,1]{2,1,0,4,3:T(8,128)(2,1)} %bitcast.110, f32[2,8,18816]{2,1,0:T(8,128)S(1)} %dynamic-slice_convert_fusion.2, f32[10,18816]{1,0:T(8,128)S(1)} %get-tuple-element.190), kind=kOutput, calls=%fused_computation.2.clone.1 | convolution fusion | flops 391372800 | bytes 4406272 | tf_op jit(solution)/shard_map/while/body/eval_jaxpr/dot_general | solution.py:44
  107.6 1.2 dynamic-slice_convert_fusion.2
  108.7 3.4 %fusion.40 = f32[10,2,8,2,32]{4,2,3,1,0:T(8,128)S(1)} fusion(bf16[2,32,18816,1,1]{2,1,0,4,3:T(8,128)(2,1)} %bitcast.110, f32[2,8,18816]{2,1,0:T(8,128)S(1)} %dynamic-slice_convert_fusion.2, f32[10,18816]{1,0:T(8,128)S(1)} %get-tuple-element.190), kind=kOutput, calls=%fused_computation.2.clone.1 | convolution fusion | flops 391372800 | bytes 4406272 | tf_op jit(solution)/shard_map/while/body/eval_jaxpr/dot_general | solution.py:44
  112.2 1.2 dynamic-slice_convert_fusion.2
  113.4 3.4 %fusion.40 = f32[10,2,8,2,32]{4,2,3,1,0:T(8,128)S(1)} fusion(bf16[2,32,18816,1,1]{2,1,0,4,3:T(8,128)(2,1)} %bitcast.110, f32[2,8,18816]{2,1,0:T(8,128)S(1)} %dynamic-slice_convert_fusion.2, f32[10,18816]{1,0:T(8,128)S(1)} %get-tuple-element.190), kind=kOutput, calls=%fused_computation.2.clone.1 | convolution fusion | flops 391372800 | bytes 4406272 | tf_op jit(solution)/shard_map/while/body/eval_jaxpr/dot_general | solution.py:44
  116.9 1.2 dynamic-slice_convert_fusion.2
  118.1 3.4 %fusion.40 = f32[10,2,8,2,32]{4,2,3,1,0:T(8,128)S(1)} fusion(bf16[2,32,18816,1,1]{2,1,0,4,3:T(8,128)(2,1)} %bitcast.110, f32[2,8,18816]{2,1,0:T(8,128)S(1)} %dynamic-slice_convert_fusion.2, f32[10,18816]{1,0:T(8,128)S(1)} %get-tuple-element.190), kind=kOutput, calls=%fused_computation.2.clone.1 | convolution fusion | flops 391372800 | bytes 4406272 | tf_op jit(solution)/shard_map/while/body/eval_jaxpr/dot_general | solution.py:44
  121.6 1.2 dynamic-slice_convert_fusion.2
  122.7 3.4 %fusion.40 = f32[10,2,8,2,32]{4,2,3,1,0:T(8,128)S(1)} fusion(bf16[2,32,18816,1,1]{2,1,0,4,3:T(8,128)(2,1)} %bitcast.110, f32[2,8,18816]{2,1,0:T(8,128)S(1)} %dynamic-slice_convert_fusion.2, f32[10,18816]{1,0:T(8,128)S(1)} %get-tuple-element.190), kind=kOutput, calls=%fused_computation.2.clone.1 | convolution fusion | flops 391372800 | bytes 4406272 | tf_op jit(solution)/shard_map/while/body/eval_jaxpr/dot_general | solution.py:44
  126.2 1.2 dynamic-slice_convert_fusion.2
  127.4 3.4 %fusion.40 = f32[10,2,8,2,32]{4,2,3,1,0:T(8,128)S(1)} fusion(bf16[2,32,18816,1,1]{2,1,0,4,3:T(8,128)(2,1)} %bitcast.110, f32[2,8,18816]{2,1,0:T(8,128)S(1)} %dynamic-slice_convert_fusion.2, f32[10,18816]{1,0:T(8,128)S(1)} %get-tuple-element.190), kind=kOutput, calls=%fused_computation.2.clone.1 | convolution fusion | flops 391372800 | bytes 4406272 | tf_op jit(solution)/shard_map/while/body/eval_jaxpr/dot_general | solution.py:44
  130.9 1.0 copy.27
  131.9 0.2 fusion.10
  132.1 30.9 %all-reduce.4.cloned.1.call-done = f32[32,10,2,64]{3,2,1,0:T(2,128)} async-done(((f32[32,10,2,64]{3,2,1,0:T(2,128)}), f32[32,10,2,64]{3,2,1,0:T(2,128)}) %all-reduce.4.cloned.1.call-update) | async-done | bytes 163856
  162.9 0.9 constant_dynamic-slice_fusion
  163.8 0.3 copy.28
  164.1 0.8 copy.32
  164.9 0.1 copy.29
  165.1 0.6 convolution_bitcast_fusion
  165.7 0.4 fusion.13
  166.0 0.4 fusion.17
  166.4 0.1 multiply_reduce_fusion
  166.5 0.1 multiply_reduce_fusion.1
  166.6 39.4 %all-reduce.1 = (f32[3,8]{0,1:T(8,128)S(1)}, f32[6]{0:T(128)S(1)}) all-reduce(f32[3,8]{0,1:T(8,128)S(1)} %multiply_reduce_fusion.1, f32[6]{0:T(128)S(1)} %multiply_reduce_fusion), channel_id=1, replica_groups=mesh['band'=8,'gvec'=4] {'band','gvec'}, use_global_device_ids=true, to_apply=%region_5.0 | all-reduce | flops 30 | bytes 240 | tf_op jit(solution)/shard_map/psum | solution.py:116
  205.9 0.7 fusion.28
  206.7 0.7 maximum_bitcast_fusion.3
  207.4 0.5 dynamic-slice_multiply_fusion
  207.9 2.6 %maximum_bitcast_fusion.1 = (f32[1,3]{1,0:T(1,128)S(1)}, f32[1,3]{1,0:T(1,128)S(1)}) fusion(f32[2]{0:T(128)S(1)} %get-tuple-element.135, f32[1]{0:T(128)} %get-tuple-element.130, f32[1]{0:T(128)} %get-tuple-element.132, f32[1]{0:T(128)} %get-tuple-element.133, f32[1]{0:T(128)} %get-tuple-element.134), kind=kLoop, calls=%fused_computation.49 | loop fusion | flops 9 | bytes 48 | tf_op jit(solution)/shard_map/stack | solution.py:78
  210.5 0.6 pad_maximum_fusion
  (37 shorter events, 0.6 us)
Async XLA Ops:
  7.2 124.7 %copy-start = (f32[4,8,8]{2,1,0:T(8,128)S(1)}, f32[4,8,8]{2,1,0:T(8,128)}, u32[]{:S(2)}) copy-start(f32[4,8,8]{2,1,0:T(8,128)} %param.17) | copy-start | bytes 3076
  7.2 86.3 %all-gather.2.cloned.1.call-start = ((), (), s32[]{:S(2)}) async-start(), calls=%async_computation | async-start | bytes 5419008 | tf_op jit(solution)/shard_map/all_gather | solution.py:96
  7.9 155.0 %all-reduce.4.cloned.1.call-start = ((), (), s32[]{:S(2)}) async-start(), calls=%async_computation.1 | async-start | bytes 655360
  93.6 38.3 %copy-start.1 = (s32[8]{0:T(128)S(1)}, s32[8]{0:T(128)}, u32[]{:S(2)}) copy-start(s32[8]{0:T(128)} %param.15) | copy-start | bytes 100
Sparse Core Ops, SparseCore 0:
  10.2 83.2 all-gather.1
  132.0 30.9 all-reduce.3
where the time goes:
time: 219 us; the launch traced here: 218 us
  waiting for transfers between devices  103 us (47%)
  blocking collectives  39.4 us (18%)
  matrix products  28.2 us (13%)
  other arithmetic  23.1 us (11%)
  between operations  14.8 us (7%)
  local copies, waits for them, and re-layouts  8.95 us (4%)
    all_gather x1, waiting for transfers between devices, body(): arrived = lax.all_gather(projectors, 'band', axis=1, tiled=True)  71.5 us
    psum x1, blocking collectives, body(): lax.psum((force_part, stress_part), ('band', 'gvec'))  39.4 us
    unnamed x3, waiting for transfers between devices  31.5 us
    dot_general x8, matrix products, intersection(): lax.dot_general(scaled, flat_waves, (((1,), (1,)), ((), ())), preferred_e...  27.4 us
    convert_element_type x8, other arithmetic, scale_block(): atom_block[None].astype(jnp.float32)  9.23 us
    mul x2, other arithmetic, cart_weights(): product = coords[first_axis] * coords[second_axis]  6.28 us
  transfers between devices with their start and end apart: 2, of which 2 were waited for; matrix products, arithmetic and copies ran while one was open for 6% of the time, Pallas kernels for 0%

commit v1 on v0

v1 whole, which is shorter than its diff:
```python
import functools
import math

import jax
import jax.numpy as jnp
from jax import lax
from jax.experimental import pallas as pl
from jax.experimental.pallas import tpu as pltpu
from jax.sharding import PartitionSpec as P

PROJ = 8
MILLER = 24
LANES = 128
ALPHA = 0.45

stress_pairs = ((0, 0), (1, 1), (2, 2), (0, 1), (0, 2), (1, 2))


def largest_divisor(total, limit):
    return max(d for d in range(1, min(total, limit) + 1) if total % d == 0)


def piece_ranges(tiles):
    ring_tiles = int(round(ALPHA * tiles))
    cuts = [0, ring_tiles // 2, ring_tiles, ring_tiles + (tiles - ring_tiles) // 2, tiles]
    return [(cuts[i] * LANES, (cuts[i + 1] - cuts[i]) * LANES) for i in range(4)]


def swap_halves(values):
    half = values.shape[1] // 2
    return jnp.concatenate([values[:, half:], values[:, :half]], axis=1)


def kernel(
    bands, slots,
    waves_hbm, proj_hbm, miller_ref, lattice_ref, occupation_ref, species_ref, count_ref, coupling_ref,
    forces_ref, stress_ref,
    gath, waves, weights, spread, overlap, first_sum, second_sum,
    local_sem, send_sem, recv_sem, small_send, small_recv, first_send, first_recv, second_send, second_recv,
):
    me = lax.axis_index("band")
    slot = lax.axis_index("gvec")
    pair = 2 if bands % 2 == 0 else 1
    ring = bands // pair
    row = me // pair
    column = me % pair
    steps = ring // 2
    width = waves.shape[1]
    tiles = width // LANES
    wave_rows = waves.shape[0]
    ranges = piece_ranges(tiles)

    own_copy = pltpu.make_async_copy(proj_hbm, gath.at[me], local_sem.at[0])
    own_copy.start()
    wave_copy = pltpu.make_async_copy(waves_hbm, waves, local_sem.at[1])
    wave_copy.start()
    barrier = pltpu.get_barrier_semaphore()
    for offset in range(1, bands):
        pl.semaphore_signal(barrier, inc=1, device_id={"band": (me + offset) % bands}, device_id_type=pl.DeviceIdType.MESH)
    for offset in range(1, slots):
        pl.semaphore_signal(barrier, inc=1, device_id={"gvec": (slot + offset) % slots}, device_id_type=pl.DeviceIdType.MESH)
    own_copy.wait()
    pl.semaphore_wait(barrier, bands + slots - 2)

    sent = []

    def block_at(direction, step, other):
        at = (row - direction * step + ring * step) % ring
        return at * pair + ((column + 1) % pair if other else column)

    def piece_copy(block, piece, target, number):
        start, size = ranges[piece]
        part = gath.at[block, :, pl.ds(start, size)]
        return pltpu.make_async_remote_copy(
            src_ref=part, dst_ref=part, send_sem=send_sem.at[number], recv_sem=recv_sem.at[piece, block],
            device_id={"band": target}, device_id_type=pl.DeviceIdType.MESH,
        )

    def send(block, piece, target):
        if ranges[piece][1] == 0:
            return
        copy = piece_copy(block, piece, target, len(sent))
        copy.start()
        sent.append(copy)

    def arrive(block, piece):
        if ranges[piece][1]:
            piece_copy(block, piece, me, 0).wait_recv()

    def neighbour(direction):
        return ((row + direction + ring) % ring) * pair + column

    across = row * pair + (column + 1) % pair

    def pieces_of(direction, step, kind):
        if step > steps or step == 0:
            return []
        if ring % 2 == 0 and step == steps:
            return [kind * 2 + (0 if direction > 0 else 1)]
        return [kind * 2, kind * 2 + 1]

    directions = (1, -1)

    def forward_ring(block, direction, step, kind):
        for piece in pieces_of(direction, step + 1, kind):
            send(block, piece, neighbour(direction))

    if pair == 2:
        for piece in (2, 3):
            send(me, piece, across)
    for kind in (0, 1):
        for direction in directions:
            forward_ring(me, direction, 0, kind)
    if pair == 2:
        for piece in (0, 1):
            send(me, piece, across)

    weight_chunk = largest_divisor(tiles, 8) * LANES

    def weight_step(step, carry):
        at = pl.ds(pl.multiple_of(step * weight_chunk, LANES), weight_chunk)
        indices = miller_ref[:, at].astype(jnp.float32)
        coords = []
        for axis in range(3):
            total = (
                indices[0:1] * lattice_ref[0, axis]
                + indices[1:2] * lattice_ref[1, axis]
                + indices[2:3] * lattice_ref[2, axis]
            )
            coords.append(total * (1.0 / MILLER))
        isotropic = (coords[0] * coords[0] + coords[1] * coords[1] + coords[2] * coords[2]) * (1.0 / 3.0)
        for axis in range(3):
            weights[axis : axis + 1, at] = coords[axis]
        for index, (first_axis, second_axis) in enumerate(stress_pairs):
            product = coords[first_axis] * coords[second_axis]
            if first_axis == second_axis:
                product = product - isotropic
            weights[3 + index : 4 + index, at] = product
        spread[:, at] = jnp.zeros((PROJ, weight_chunk), jnp.float32)
        return carry

    lax.fori_loop(0, width // weight_chunk, weight_step, 0)
    wave_copy.wait()

    chunk = largest_divisor(tiles, 24) * LANES
    lane = lax.broadcasted_iota(jnp.int32, (8, LANES), 1)
    sublane = lax.broadcasted_iota(jnp.int32, (8, LANES), 0)
    half_lane = lax.broadcasted_iota(jnp.int32, (PROJ, wave_rows), 1) < wave_rows // 2
    sign = jnp.where(half_lane, 1.0, -1.0).astype(jnp.float32)
    occupied = jnp.concatenate([occupation_ref[...], occupation_ref[...]], axis=1)

    def small_copy(block, offset):
        part = overlap.at[block, slot]
        return pltpu.make_async_remote_copy(
            src_ref=part, dst_ref=part, send_sem=small_send.at[block, offset - 1],
            recv_sem=small_recv.at[block, offset - 1],
            device_id={"gvec": (slot + offset) % slots}, device_id_type=pl.DeviceIdType.MESH,
        )

    def small_arrival(block, offset):
        part = overlap.at[block, (slot + slots - offset) % slots]
        return pltpu.make_async_remote_copy(
            src_ref=part, dst_ref=part, send_sem=small_send.at[block, offset - 1],
            recv_sem=small_recv.at[block, offset - 1],
            device_id={"gvec": (slot + offset) % slots}, device_id_type=pl.DeviceIdType.MESH,
        )

    def project(block):
        def body(step, total):
            at = pl.ds(pl.multiple_of(step * chunk, LANES), chunk)
            return total + lax.dot_general(
                gath[block, :, at], waves[:, at], (((1,), (1,)), ((), ())), preferred_element_type=jnp.float32
            )

        product = lax.fori_loop(0, width // chunk, body, jnp.zeros((2 * PROJ, wave_rows), jnp.float32))
        becp = product[:PROJ] + sign * swap_halves(product[PROJ:])
        overlap[block, slot] = becp
        for offset in range(1, slots):
            small_copy(block, offset).start()

    def finish(block, part):
        for offset in range(1, slots):
            small_arrival(block, offset).wait_recv()
        becp = overlap[block, 0]
        for peer in range(1, slots):
            becp = becp + overlap[block, peer]
        matrix = jnp.zeros((PROJ, PROJ), jnp.float32)
        for kind in range(coupling_ref.shape[0]):
            matrix = matrix + jnp.where(species_ref[block] == kind, 1.0, 0.0) * coupling_ref[kind]
        active_row = lax.broadcasted_iota(jnp.int32, (PROJ, PROJ), 0) < count_ref[block]
        active_column = lax.broadcasted_iota(jnp.int32, (PROJ, PROJ), 1) < count_ref[block]
        matrix = jnp.where(active_row & active_column, matrix, 0.0)
        mixed = matrix[:, 0:1] * becp[0:1]
        for index in range(1, PROJ):
            mixed = mixed + matrix[:, index : index + 1] * becp[index : index + 1]
        mixed = mixed * occupied
        factors = jnp.concatenate([mixed, -sign * swap_halves(mixed)], axis=0)
        high = factors.astype(jnp.bfloat16)
        low = (factors - high.astype(jnp.float32)).astype(jnp.bfloat16)
        stacked = jnp.concatenate([high, low], axis=0)

        def body(step, sums):
            at = pl.ds(pl.multiple_of(step * chunk, LANES), chunk)
            both = jnp.dot(stacked, waves[:, at], preferred_element_type=jnp.float32)
            both = both[: 2 * PROJ] + both[2 * PROJ :]
            projectors = gath[block, :, at].astype(jnp.float32)
            proj_real, proj_imag = projectors[:PROJ], projectors[PROJ:]
            sum_real, sum_imag = both[:PROJ], both[PROJ:]
            imag_part = proj_real * sum_imag - proj_imag * sum_real
            spread[:, at] += proj_real * sum_real + proj_imag * sum_imag
            new = []
            for axis in range(3):
                weighted = imag_part * weights[axis : axis + 1, at]
                total = sums[axis]
                for tile in range(chunk // LANES):
                    total = total + weighted[:, tile * LANES : (tile + 1) * LANES]
                new.append(total)
            return tuple(new)

        zero = jnp.zeros((PROJ, LANES), jnp.float32)
        sums = lax.fori_loop(0, width // chunk, body, (zero, zero, zero))
        for axis in range(3):
            value = jnp.sum(jnp.sum(sums[axis], axis=0, keepdims=True), axis=1, keepdims=True)
            part = part + jnp.where((sublane == axis) & (lane == block), value, 0.0)
        return part

    state = {"part": jnp.zeros((8, LANES), jnp.float32), "waiting": None, "blocks": []}

    def work(block):
        project(block)
        state["blocks"].append(block)
        if state["waiting"] is not None:
            state["part"] = finish(state["waiting"], state["part"])
        state["waiting"] = block

    def ring_blocks(step, other):
        chosen = [block_at(1, step, other)]
        if not (ring % 2 == 0 and step == steps):
            chosen.append(block_at(-1, step, other))
        return chosen

    def take_ring(step, other, kind):
        for direction in directions:
            block = block_at(direction, step, other)
            for piece in pieces_of(direction, step, kind):
                arrive(block, piece)
                if piece in pieces_of(direction, step + 1, kind):
                    send(block, piece, neighbour(direction))
                if kind == 0 and not other and pair == 2:
                    send(block, piece, across)

    def take_across(step):
        for block in ring_blocks(step, True):
            for piece in (0, 1):
                arrive(block, piece)

    work(me)
    if pair == 2:
        for piece in (2, 3):
            arrive(across, piece)
            for direction in directions:
                if piece in pieces_of(direction, 1, 1):
                    send(across, piece, neighbour(direction))
        for piece in (0, 1):
            arrive(across, piece)
        work(across)
    for step in range(1, steps + 1):
        take_ring(step, False, 0)
        if step > 1 and pair == 2:
            take_across(step - 1)
            for block in ring_blocks(step - 1, True):
                work(block)
        take_ring(step, False, 1)
        if pair == 2:
            take_ring(step, True, 1)
        for block in ring_blocks(step, False):
            work(block)
    if pair == 2 and steps:
        take_across(steps)
        for block in ring_blocks(steps, True):
            work(block)
    part = finish(state["waiting"], state["part"])

    def stress_step(step, sums):
        at = pl.ds(pl.multiple_of(step * chunk, LANES), chunk)
        density = jnp.sum(spread[:, at], axis=0, keepdims=True)
        weighted = weights[:, at] * density
        for tile in range(chunk // LANES):
            sums = sums + weighted[:, tile * LANES : (tile + 1) * LANES]
        return sums

    weights[9:16, :] = jnp.zeros((7, width), jnp.float32)
    stress_sums = lax.fori_loop(0, width // chunk, stress_step, jnp.zeros((16, LANES), jnp.float32))
    stress_values = jnp.sum(stress_sums, axis=1, keepdims=True)[3:11]
    part = jnp.where(lane == LANES - 1, stress_values, part)

    def exchange(values, store, axis_name, index, count, send_sems, recv_sems):
        store[index] = values
        copies = []
        for offset in range(1, count):
            mine = store.at[index]
            copy = pltpu.make_async_remote_copy(
                src_ref=mine, dst_ref=mine, send_sem=send_sems.at[offset - 1], recv_sem=recv_sems.at[offset - 1],
                device_id={axis_name: (index + offset) % count}, device_id_type=pl.DeviceIdType.MESH,
            )
            copy.start()
            copies.append(copy)
        for offset in range(1, count):
            theirs = store.at[(index + count - offset) % count]
            pltpu.make_async_remote_copy(
                src_ref=theirs, dst_ref=theirs, send_sem=send_sems.at[offset - 1], recv_sem=recv_sems.at[offset - 1],
                device_id={axis_name: (index + offset) % count}, device_id_type=pl.DeviceIdType.MESH,
            ).wait_recv()
        total = store[0]
        for other in range(1, count):
            total = total + store[other]
        return total, copies

    total, first_copies = exchange(part, first_sum, "gvec", slot, slots, first_send, first_recv)
    total, second_copies = exchange(total, second_sum, "band", me, bands, second_send, second_recv)

    band_total = bands * (wave_rows // 2)
    force_scale = 2.0 / (PROJ * math.sqrt(band_total))
    stress_scale = 1.0 / (PROJ * math.sqrt(bands * band_total))
    own_force = jnp.sum(jnp.where(lane == me, total, 0.0), axis=1, keepdims=True)
    forces_ref[...] = own_force[:3] * force_scale
    line = lax.broadcasted_iota(jnp.int32, (3, 3), 0)
    place = lax.broadcasted_iota(jnp.int32, (3, 3), 1)
    matrix = jnp.zeros((3, 3), jnp.float32)
    for index, (first_axis, second_axis) in enumerate(stress_pairs):
        here = ((line == first_axis) & (place == second_axis)) | ((line == second_axis) & (place == first_axis))
        matrix = jnp.where(here, total[index : index + 1, LANES - 1 : LANES] * stress_scale, matrix)
    stress_ref[...] = matrix

    for copy in sent + first_copies + second_copies:
        copy.wait_send()
    for block in state["blocks"]:
        for offset in range(1, slots):
            small_copy(block, offset).wait_send()


def body(bands, slots, wave_coeffs, projectors, miller_index, lattice, occupation, species, proj_count, coupling):
    band_count, width = wave_coeffs.shape[1:]
    assert projectors.shape[1] == PROJ and width % LANES == 0 and bands < LANES
    vmem = pl.BlockSpec(memory_space=pltpu.VMEM)
    smem = pl.BlockSpec(memory_space=pltpu.SMEM)
    hbm = pl.BlockSpec(memory_space=pl.ANY)
    dma = pltpu.SemaphoreType.DMA
    sends = 12 * bands
    return pl.pallas_call(
        functools.partial(kernel, bands, slots),
        out_shape=(jax.ShapeDtypeStruct((3, 1), jnp.float32), jax.ShapeDtypeStruct((3, 3), jnp.float32)),
        in_specs=[hbm, hbm, vmem, smem, vmem, smem, smem, vmem],
        out_specs=(vmem, vmem),
        scratch_shapes=[
            pltpu.VMEM((bands, 2 * PROJ, width), jnp.bfloat16),
            pltpu.VMEM((2 * band_count, width), jnp.bfloat16),
            pltpu.VMEM((16, width), jnp.float32),
            pltpu.VMEM((PROJ, width), jnp.float32),
            pltpu.VMEM((bands, slots, PROJ, 2 * band_count), jnp.float32),
            pltpu.VMEM((slots, 8, LANES), jnp.float32),
            pltpu.VMEM((bands, 8, LANES), jnp.float32),
            dma((2,)),
            dma((sends,)),
            dma((4, bands)),
            dma((bands, slots - 1)),
            dma((bands, slots - 1)),
            dma((slots - 1,)),
            dma((slots - 1,)),
            dma((bands - 1,)),
            dma((bands - 1,)),
        ],
        compiler_params=pltpu.CompilerParams(collective_id=0, has_side_effects=True, vmem_limit_bytes=56 * 2**20),
    )(
        wave_coeffs.reshape(2 * band_count, width),
        projectors.reshape(2 * PROJ, width),
        miller_index,
        lattice,
        occupation.reshape(1, band_count),
        species,
        proj_count,
        coupling,
    )


def solution(mesh):
    return jax.shard_map(
        functools.partial(body, mesh.shape["band"], mesh.shape["gvec"]),
        mesh=mesh,
        in_specs=(
            P(None, "band", "gvec"),
            P(None, "band", "gvec"),
            P(None, "gvec"),
            P(),
            P("band"),
            P(),
            P(),
            P(),
        ),
        out_specs=(P(None, "band"), P()),
        check_vma=False,
    )
```

time: 219 us -> 91.2 us (0.42)
  waiting for transfers between devices: 103 us -> 0 us
  Pallas kernels: 0 us -> 87.8 us
  blocking collectives: 39.4 us -> 0 us
  matrix products: 28.2 us -> 0 us
  other arithmetic: 23.1 us -> 0 us
  between operations: 14.8 us -> 0.64 us
  local copies, waits for them, and re-layouts: 8.95 us -> 2.49 us
    pallas_call x0 -> x1, Pallas kernels: none -> 87.8 us  [body(): pl.pallas_call(functools.partial(kernel, bands, slots), out_shape=(jax.Sh...]
    all_gather x1 -> x0, waiting for transfers between devices: 71.5 us -> none  [body(): arrived = lax.all_gather(projectors, 'band', axis=1, tiled=True)]
    psum x1 -> x0, blocking collectives: 39.4 us -> none  [body(): lax.psum((force_part, stress_part), ('band', 'gvec'))]
    unnamed x3 -> x0, waiting for transfers between devices: 31.5 us -> none
    dot_general x10 -> x0, matrix products: 28.2 us -> none  [the longest x8 27.4 us: intersection(): lax.dot_general(scaled, flat_waves, (((1,), (1,)), ((), ())), preferred_e...]
    convert_element_type x10 -> x0, other arithmetic: 11 us -> none  [the longest x8 9.23 us: scale_block(): atom_block[None].astype(jnp.float32)]
    mul x4 -> x0, other arithmetic: 6.8 us -> none  [the longest x2 6.28 us: cart_weights(): product = coords[first_axis] * coords[second_axis]]
    another operation x3 -> x0, other arithmetic: 3.9 us -> none  [stress_matrix(): jnp.stack([jnp.stack([values[0], values[3], values[4]]), jnp.stack([value...]
  transfers between devices with their start and end apart: 2 -> 0, of which waited for: 2 -> 0; matrix products, arithmetic and copies ran while one was open for 6% -> 0% of each run, Pallas kernels for 0% -> 0%
where the time goes in v1:
time: 91.2 us; the launch traced here: 91 us
  Pallas kernels  87.8 us (96%)
  local copies, waits for them, and re-layouts  2.49 us (3%)
    pallas_call x1, Pallas kernels, body(): pl.pallas_call(functools.partial(kernel, bands, slots), out_shape=(jax.Sh...  87.8 us

profile of v1, /device:TPU:0, one launch (start us, length us, event | category | flops | bytes accessed | tf_op | source)
XLA Modules:
  0.0 91.0 jit_solution(11349467887081961364)
XLA Ops:
  0.6 87.8 %shard_map.95 = (f32[3,1]{1,0:T(4,128)}, f32[3,3]{1,0:T(4,128)}) custom-call(bf16[64,18816]{1,0:T(8,128)(2,1)} %bitcast.3, bf16[16,18816]{1,0:T(8,128)(2,1)} %bitcast.4, s32[3,18816]{1,0:T(4,128)} %miller_ref.1, f32[3,3]{1,0:T(4,128)} %lattice_ref.1, f32[1,32]{1,0:T(1,128)} %bitcast.5, s32[8]{0:T(128)} %species_ref.1, s32[8]{0:T(128)} %count_ref.1, ...), custom_call_target="tpu_custom_call" | custom-call | tf_op jit(solution)/shard_map/pallas_call | solution.py:350
  88.5 1.3 %copy.10 = f32[3,1]{0,1:T(1,128)} copy(f32[3,1]{1,0:T(4,128)} %get-tuple-element.2) | data formatting | bytes 24 | tf_op jit(solution)/shard_map/pallas_call | solution.py:350
  89.8 1.2 %copy.12 = f32[3,3]{1,0:T(4,128)} copy(f32[3,3]{1,0:T(4,128)} %get-tuple-element.7) | data formatting | bytes 72

commit v2 on v0

v2 whole, which is shorter than its diff:
```python
import functools
import math

import jax
import jax.numpy as jnp
from jax import lax
from jax.experimental import pallas as pl
from jax.experimental.pallas import tpu as pltpu
from jax.sharding import PartitionSpec as P

PROJ = 8
MILLER = 24
LANES = 128
CHUNK_TILES = 40
PIECES = 2

stress_pairs = ((0, 0), (1, 1), (2, 2), (0, 1), (0, 2), (1, 2))
MESH = pl.DeviceIdType.MESH


def largest_divisor(total, limit):
    return max(d for d in range(1, min(total, limit) + 1) if total % d == 0)


def swap_halves(values, group):
    half = group // 2
    parts = []
    for start in range(0, values.shape[1], group):
        parts += [values[:, start + half : start + group], values[:, start : start + half]]
    return jnp.concatenate(parts, axis=1)


def kernel(
    bands, slots,
    waves_hbm, proj_hbm, miller_ref, lattice_ref, occupation_ref, species_ref, count_ref, coupling_ref,
    forces_ref, stress_ref,
    gath, waves, weights, spread, overlap, first_sum, second_sum, filling, part_ref,
    local_sem, send_sem, recv_sem, pair_send, pair_recv, small_send, small_recv,
    first_send, first_recv, second_send, second_recv,
):
    me = lax.axis_index("band")
    slot = lax.axis_index("gvec")
    pair = waves.shape[0]
    line = bands // pair
    row = me // pair
    column = me % pair
    other = (column + 1) % pair
    across = row * pair + other
    group = waves.shape[1]
    width = waves.shape[2]
    held_tiles = width // LANES
    skip = waves_hbm.shape[1] // LANES - held_tiles
    begin = pl.multiple_of(column * skip * LANES, LANES)
    other_begin = pl.multiple_of(other * skip * LANES, LANES)
    cuts = [held_tiles * i // PIECES * LANES for i in range(PIECES + 1)]
    peers = pair * slots
    rank = column * slots + slot

    def peer_id(index):
        return {"band": row * pair + index // slots, "gvec": index % slots}

    def line_id(position):
        return {"band": position * pair + column, "gvec": slot}

    own_copy = pltpu.make_async_copy(proj_hbm.at[:, pl.ds(begin, width)], gath.at[row, column], local_sem.at[0])
    own_copy.start()
    wave_copy = pltpu.make_async_copy(waves_hbm.at[:, pl.ds(begin, width)], waves.at[column], local_sem.at[1])
    wave_copy.start()
    barrier = pltpu.get_barrier_semaphore()
    for offset in range(1, peers):
        pl.semaphore_signal(barrier, inc=1, device_id=peer_id((rank + offset) % peers), device_id_type=MESH)
    for offset in range(1, line):
        pl.semaphore_signal(barrier, inc=1, device_id=line_id((row + offset) % line), device_id_type=MESH)
    lanes = occupation_ref[...]
    tiled = jnp.concatenate([lanes, lanes] * pair, axis=1)
    where_lane = lax.broadcasted_iota(jnp.int32, (8, pair * group), 1)
    filling[column] = jnp.where(where_lane // group == column, jnp.broadcast_to(tiled, where_lane.shape), 0.0)
    pl.semaphore_wait(barrier, peers + line - 2)

    pair_copies = []

    def pair_copy(source, target, number):
        return pltpu.make_async_remote_copy(
            src_ref=source, dst_ref=target, send_sem=pair_send.at[number], recv_sem=pair_recv.at[number],
            device_id={"band": across, "gvec": slot}, device_id_type=MESH,
        )

    if pair == 2:
        for piece in range(PIECES):
            start, size = cuts[piece], cuts[piece + 1] - cuts[piece]
            pair_copies.append(pair_copy(
                proj_hbm.at[:, pl.ds(pl.multiple_of(other_begin + start, LANES), size)],
                gath.at[row, column, :, pl.ds(start, size)], piece,
            ))
        pair_copies.append(pair_copy(filling.at[column], filling.at[column], PIECES))
        pair_copies.append(pair_copy(waves_hbm.at[:, pl.ds(other_begin, width)], waves.at[column], PIECES + 1))
        for copy in pair_copies:
            copy.start()

    def line_copy(position, source_column, piece, way, target):
        start, size = cuts[piece], cuts[piece + 1] - cuts[piece]
        part = gath.at[position, source_column, :, pl.ds(start, size)]
        return pltpu.make_async_remote_copy(
            src_ref=part, dst_ref=part, send_sem=send_sem.at[way, position, source_column, piece],
            recv_sem=recv_sem.at[position, source_column, piece],
            device_id=line_id(target), device_id_type=MESH,
        )

    def has_next(way):
        return row < line - 1 if way == 0 else row > 0

    def holds(way, step):
        return row >= step if way == 0 else row + step < line

    def origin(way, step):
        return row - step if way == 0 else row + step

    def following(way):
        return row + 1 if way == 0 else row - 1

    def pass_on(position, source_column, piece):
        for way in (0, 1):
            @pl.when(has_next(way))
            def _():
                line_copy(position, source_column, piece, way, following(way)).start()

    own_copy.wait()
    for piece in range(PIECES):
        pass_on(row, column, piece)

    weight_chunk = largest_divisor(held_tiles, 8) * LANES

    def weight_step(step, carry):
        at = pl.ds(pl.multiple_of(step * weight_chunk, LANES), weight_chunk)
        indices = miller_ref[:, pl.ds(pl.multiple_of(begin + step * weight_chunk, LANES), weight_chunk)].astype(jnp.float32)
        coords = []
        for axis in range(3):
            total = (
                indices[0:1] * lattice_ref[0, axis]
                + indices[1:2] * lattice_ref[1, axis]
                + indices[2:3] * lattice_ref[2, axis]
            )
            coords.append(total * (1.0 / MILLER))
        isotropic = (coords[0] * coords[0] + coords[1] * coords[1] + coords[2] * coords[2]) * (1.0 / 3.0)
        for axis in range(3):
            weights[axis : axis + 1, at] = coords[axis]
        for index, (first_axis, second_axis) in enumerate(stress_pairs):
            product = coords[first_axis] * coords[second_axis]
            if first_axis == second_axis:
                product = product - isotropic
            weights[3 + index : 4 + index, at] = product
        weights[9:16, at] = jnp.zeros((7, weight_chunk), jnp.float32)
        spread[:, at] = jnp.zeros((PROJ, weight_chunk), jnp.float32)
        return carry

    def make_weights():
        lax.fori_loop(0, width // weight_chunk, weight_step, 0)

    if pair == 2:
        for piece in range(PIECES):
            start, size = cuts[piece], cuts[piece + 1] - cuts[piece]
            part = gath.at[row, other, :, pl.ds(start, size)]
            pair_copy(part, part, piece).wait_recv()
            pass_on(row, other, piece)
    make_weights()
    part_ref[...] = jnp.zeros_like(part_ref)

    chunk = largest_divisor(held_tiles, CHUNK_TILES) * LANES
    rows = pair * PROJ
    lane = lax.broadcasted_iota(jnp.int32, (8, LANES), 1)
    sublane = lax.broadcasted_iota(jnp.int32, (8, LANES), 0)
    first_half = lax.broadcasted_iota(jnp.int32, (PROJ, pair * group), 1) % group < group // 2
    sign = jnp.where(first_half, 1.0, -1.0).astype(jnp.float32)

    def small_copy(position, offset, source, target):
        piece = overlap.at[position, source]
        return pltpu.make_async_remote_copy(
            src_ref=piece, dst_ref=piece, send_sem=small_send.at[position, offset - 1],
            recv_sem=small_recv.at[position, offset - 1], device_id=peer_id(target), device_id_type=MESH,
        )

    def outgoing(position, offset):
        return small_copy(position, offset, rank, (rank + offset) % peers)

    def incoming(position, offset):
        return small_copy(position, offset, (rank + peers - offset) % peers, (rank + offset) % peers)

    def block_rows(position, at):
        return jnp.concatenate([gath[position, index, :, at] for index in range(pair)], axis=0)

    def wave_chunk(at):
        return jnp.concatenate([waves[index, :, at] for index in range(pair)], axis=0)

    def project(position):
        def body(step, total):
            at = pl.ds(pl.multiple_of(step * chunk, LANES), chunk)
            return total + lax.dot_general(
                block_rows(position, at), wave_chunk(at), (((1,), (1,)), ((), ())), preferred_element_type=jnp.float32
            )

        product = lax.fori_loop(0, width // chunk, body, jnp.zeros((2 * rows, pair * group), jnp.float32))
        becp = []
        for index in range(pair):
            base = 2 * PROJ * index
            becp.append(product[base : base + PROJ] + sign * swap_halves(product[base + PROJ : base + 2 * PROJ], group))
        overlap[position, rank] = jnp.concatenate(becp, axis=0)
        for offset in range(1, peers):
            outgoing(position, offset).start()

    def atom_matrix(atom):
        matrix = jnp.zeros((PROJ, PROJ), jnp.float32)
        for kind in range(coupling_ref.shape[0]):
            matrix = matrix + jnp.where(species_ref[atom] == kind, 1.0, 0.0) * coupling_ref[kind]
        active_row = lax.broadcasted_iota(jnp.int32, (PROJ, PROJ), 0) < count_ref[atom]
        active_column = lax.broadcasted_iota(jnp.int32, (PROJ, PROJ), 1) < count_ref[atom]
        return jnp.where(active_row & active_column, matrix, 0.0)

    def finish(position):
        for offset in range(1, peers):
            incoming(position, offset).wait_recv()
        becp = overlap[position, 0]
        for peer in range(1, peers):
            becp = becp + overlap[position, peer]
        occupied = filling[0]
        for index in range(1, pair):
            occupied = occupied + filling[index]
        factors = []
        for index in range(pair):
            matrix = atom_matrix(position * pair + index)
            base = PROJ * index
            mixed = matrix[:, 0:1] * becp[base : base + 1]
            for term in range(1, PROJ):
                mixed = mixed + matrix[:, term : term + 1] * becp[base + term : base + term + 1]
            mixed = mixed * occupied
            factors += [mixed, -sign * swap_halves(mixed, group)]
        factors = jnp.concatenate(factors, axis=0)
        high = factors.astype(jnp.bfloat16)
        low = (factors - high.astype(jnp.float32)).astype(jnp.bfloat16)
        stacked = jnp.concatenate([high, low], axis=0)

        def body(step, sums):
            at = pl.ds(pl.multiple_of(step * chunk, LANES), chunk)
            both = jnp.dot(stacked, wave_chunk(at), preferred_element_type=jnp.float32)
            both = both[: 2 * rows] + both[2 * rows :]
            density = spread[:, at]
            new = []
            for index in range(pair):
                base = 2 * PROJ * index
                projectors = gath[position, index, :, at].astype(jnp.float32)
                proj_real, proj_imag = projectors[:PROJ], projectors[PROJ:]
                sum_real, sum_imag = both[base : base + PROJ], both[base + PROJ : base + 2 * PROJ]
                imag_part = proj_real * sum_imag - proj_imag * sum_real
                density = density + proj_real * sum_real + proj_imag * sum_imag
                for axis in range(3):
                    weighted = imag_part * weights[axis : axis + 1, at]
                    total = sums[index * 3 + axis]
                    for tile in range(chunk // LANES):
                        total = total + weighted[:, tile * LANES : (tile + 1) * LANES]
                    new.append(total)
            spread[:, at] = density
            return tuple(new)

        zero = jnp.zeros((PROJ, LANES), jnp.float32)
        sums = lax.fori_loop(0, width // chunk, body, (zero,) * (3 * pair))
        part = part_ref[...]
        for index in range(pair):
            for axis in range(3):
                value = jnp.sum(jnp.sum(sums[index * 3 + axis], axis=0, keepdims=True), axis=1, keepdims=True)
                part = part + jnp.where((sublane == axis) & (lane == position * pair + index), value, 0.0)
        part_ref[...] = part

    def take(step):
        for source in range(pair):
            for piece in range(PIECES):
                for way in (0, 1):
                    @pl.when(holds(way, step))
                    def _():
                        line_copy(origin(way, step), source, piece, way, row).wait_recv()

                        @pl.when(has_next(way))
                        def _():
                            line_copy(origin(way, step), source, piece, way, following(way)).start()

    def each(step, action):
        if step == 0:
            action(row)
            return
        for way in (0, 1):
            @pl.when(holds(way, step))
            def _():
                action(origin(way, step))

    for step in range(1, line - 1):
        take(step)
    wave_copy.wait()
    if pair == 2:
        pair_copy(filling.at[other], filling.at[other], PIECES).wait_recv()
        pair_copy(waves.at[other], waves.at[other], PIECES + 1).wait_recv()
        if held_tiles > skip:
            shared = pl.ds(0, (held_tiles - skip) * LANES)
            keep = jnp.where(column == 0, 1.0, 0.0).astype(jnp.bfloat16)
            for index in range(pair):
                waves[index, :, shared] = waves[index, :, shared] * keep
    for step in range(line):
        if step and step == line - 1:
            take(step)
        each(step, project)
        if step:
            each(step - 1, finish)
    each(line - 1, finish)

    def stress_step(step, sums):
        at = pl.ds(pl.multiple_of(step * chunk, LANES), chunk)
        density = jnp.sum(spread[:, at], axis=0, keepdims=True)
        weighted = weights[:, at] * density
        for tile in range(chunk // LANES):
            sums = sums + weighted[:, tile * LANES : (tile + 1) * LANES]
        return sums

    stress_sums = lax.fori_loop(0, width // chunk, stress_step, jnp.zeros((16, LANES), jnp.float32))
    stress_values = jnp.sum(stress_sums, axis=1, keepdims=True)[3:11]
    part = jnp.where(lane == LANES - 1, stress_values, part_ref[...])

    def exchange(values, store, target_of, index, count, send_sems, recv_sems):
        store[index] = values
        copies = []

        def part_copy(held, offset):
            return pltpu.make_async_remote_copy(
                src_ref=store.at[held], dst_ref=store.at[held], send_sem=send_sems.at[offset - 1],
                recv_sem=recv_sems.at[offset - 1], device_id=target_of((index + offset) % count), device_id_type=MESH,
            )

        for offset in range(1, count):
            copies.append(part_copy(index, offset))
            copies[-1].start()
        for offset in range(1, count):
            part_copy((index + count - offset) % count, offset).wait_recv()
        total = store[0]
        for held in range(1, count):
            total = total + store[held]
        return total, copies

    total, first_copies = exchange(part, first_sum, peer_id, rank, peers, first_send, first_recv)
    total, second_copies = exchange(total, second_sum, line_id, row, line, second_send, second_recv)

    band_total = bands * (group // 2)
    force_scale = 2.0 / (PROJ * math.sqrt(band_total))
    stress_scale = 1.0 / (PROJ * math.sqrt(bands * band_total))
    own_force = jnp.sum(jnp.where(lane == me, total, 0.0), axis=1, keepdims=True)
    forces_ref[...] = own_force[:3] * force_scale
    down = lax.broadcasted_iota(jnp.int32, (3, 3), 0)
    along = lax.broadcasted_iota(jnp.int32, (3, 3), 1)
    matrix = jnp.zeros((3, 3), jnp.float32)
    for index, (first_axis, second_axis) in enumerate(stress_pairs):
        here = ((down == first_axis) & (along == second_axis)) | ((down == second_axis) & (along == first_axis))
        matrix = jnp.where(here, total[index : index + 1, LANES - 1 : LANES] * stress_scale, matrix)
    stress_ref[...] = matrix

    for copy in pair_copies + first_copies + second_copies:
        copy.wait_send()
    for way in (0, 1):
        for step in range(line - 1):
            for source in range(pair):
                for piece in range(PIECES):
                    @pl.when(has_next(way) & holds(way, step))
                    def _():
                        line_copy(origin(way, step), source, piece, way, following(way)).wait_send()
    for position in range(line):
        for offset in range(1, peers):
            outgoing(position, offset).wait_send()


def body(bands, slots, wave_coeffs, projectors, miller_index, lattice, occupation, species, proj_count, coupling):
    band_count, width = wave_coeffs.shape[1:]
    assert projectors.shape[1] == PROJ and width % LANES == 0 and bands < LANES
    vmem = pl.BlockSpec(memory_space=pltpu.VMEM)
    smem = pl.BlockSpec(memory_space=pltpu.SMEM)
    hbm = pl.BlockSpec(memory_space=pl.ANY)
    dma = pltpu.SemaphoreType.DMA
    pair = 2 if bands % 2 == 0 else 1
    line = bands // pair
    peers = pair * slots
    held = -(-(width // LANES) // pair) * LANES
    return pl.pallas_call(
        functools.partial(kernel, bands, slots),
        out_shape=(jax.ShapeDtypeStruct((3, 1), jnp.float32), jax.ShapeDtypeStruct((3, 3), jnp.float32)),
        in_specs=[hbm, hbm, vmem, smem, vmem, smem, smem, vmem],
        out_specs=(vmem, vmem),
        scratch_shapes=[
            pltpu.VMEM((line, pair, 2 * PROJ, held), jnp.bfloat16),
            pltpu.VMEM((pair, 2 * band_count, held), jnp.bfloat16),
            pltpu.VMEM((16, held), jnp.float32),
            pltpu.VMEM((PROJ, held), jnp.float32),
            pltpu.VMEM((line, peers, pair * PROJ, pair * 2 * band_count), jnp.float32),
            pltpu.VMEM((peers, 8, LANES), jnp.float32),
            pltpu.VMEM((line, 8, LANES), jnp.float32),
            pltpu.VMEM((pair, 8, pair * 2 * band_count), jnp.float32),
            pltpu.VMEM((8, LANES), jnp.float32),
            dma((2,)),
            dma((2, line, pair, PIECES)),
            dma((line, pair, PIECES)),
            dma((PIECES + 2,)),
            dma((PIECES + 2,)),
            dma((line, peers - 1)),
            dma((line, peers - 1)),
            dma((peers - 1,)),
            dma((peers - 1,)),
            dma((line - 1,)),
            dma((line - 1,)),
        ],
        compiler_params=pltpu.CompilerParams(collective_id=0, has_side_effects=True, vmem_limit_bytes=56 * 2**20),
    )(
        wave_coeffs.reshape(2 * band_count, width),
        projectors.reshape(2 * PROJ, width),
        miller_index,
        lattice,
        occupation.reshape(1, band_count),
        species,
        proj_count,
        coupling,
    )


def solution(mesh):
    return jax.shard_map(
        functools.partial(body, mesh.shape["band"], mesh.shape["gvec"]),
        mesh=mesh,
        in_specs=(
            P(None, "band", "gvec"),
            P(None, "band", "gvec"),
            P(None, "gvec"),
            P(),
            P("band"),
            P(),
            P(),
            P(),
        ),
        out_specs=(P(None, "band"), P()),
        check_vma=False,
    )
```

time: 219 us -> 66.3 us (0.30)
  waiting for transfers between devices: 103 us -> 0 us
  Pallas kernels: 0 us -> 63 us
  blocking collectives: 39.4 us -> 0 us
  matrix products: 28.2 us -> 0 us
  other arithmetic: 23.1 us -> 0 us
  between operations: 14.8 us -> 0.64 us
  local copies, waits for them, and re-layouts: 8.95 us -> 2.49 us
    all_gather x1 -> x0, waiting for transfers between devices: 71.5 us -> none  [body(): arrived = lax.all_gather(projectors, 'band', axis=1, tiled=True)]
    pallas_call x0 -> x1, Pallas kernels: none -> 63 us  [body(): pl.pallas_call(functools.partial(kernel, bands, slots), out_shape=(jax.Sh...]
    psum x1 -> x0, blocking collectives: 39.4 us -> none  [body(): lax.psum((force_part, stress_part), ('band', 'gvec'))]
    unnamed x3 -> x0, waiting for transfers between devices: 31.5 us -> none
    dot_general x10 -> x0, matrix products: 28.2 us -> none  [the longest x8 27.4 us: intersection(): lax.dot_general(scaled, flat_waves, (((1,), (1,)), ((), ())), preferred_e...]
    convert_element_type x10 -> x0, other arithmetic: 11 us -> none  [the longest x8 9.23 us: scale_block(): atom_block[None].astype(jnp.float32)]
    mul x4 -> x0, other arithmetic: 6.8 us -> none  [the longest x2 6.28 us: cart_weights(): product = coords[first_axis] * coords[second_axis]]
    another operation x3 -> x0, other arithmetic: 3.9 us -> none  [stress_matrix(): jnp.stack([jnp.stack([values[0], values[3], values[4]]), jnp.stack([value...]
  transfers between devices with their start and end apart: 2 -> 0, of which waited for: 2 -> 0; matrix products, arithmetic and copies ran while one was open for 6% -> 0% of each run, Pallas kernels for 0% -> 0%
where the time goes in v2:
time: 66.3 us; the launch traced here: 66.1 us
  Pallas kernels  63 us (95%)
  local copies, waits for them, and re-layouts  2.49 us (4%)
    pallas_call x1, Pallas kernels, body(): pl.pallas_call(functools.partial(kernel, bands, slots), out_shape=(jax.Sh...  63 us

profile of v2, /device:TPU:0, one launch (start us, length us, event | category | flops | bytes accessed | tf_op | source)
XLA Modules:
  0.0 66.1 jit_solution(9150379683868096504)
XLA Ops:
  0.6 63.0 %shard_map.95 = (f32[3,1]{1,0:T(4,128)}, f32[3,3]{1,0:T(4,128)}) custom-call(bf16[64,18816]{1,0:T(8,128)(2,1)} %bitcast.3, bf16[16,18816]{1,0:T(8,128)(2,1)} %bitcast.4, s32[3,18816]{1,0:T(4,128)} %miller_ref.1, f32[3,3]{1,0:T(4,128)} %lattice_ref.1, f32[1,32]{1,0:T(1,128)} %bitcast.5, s32[8]{0:T(128)} %species_ref.1, s32[8]{0:T(128)} %count_ref.1, ...), custom_call_target="tpu_custom_call" | custom-call | tf_op jit(solution)/shard_map/pallas_call | solution.py:385
  63.6 1.3 %copy.10 = f32[3,1]{0,1:T(1,128)} copy(f32[3,1]{1,0:T(4,128)} %get-tuple-element.2) | data formatting | bytes 24 | tf_op jit(solution)/shard_map/pallas_call | solution.py:385
  64.9 1.2 %copy.12 = f32[3,3]{1,0:T(4,128)} copy(f32[3,3]{1,0:T(4,128)} %get-tuple-element.7) | data formatting | bytes 72

commit v3 on v2

--- a/solution.py
+++ b/solution.py
@@ -32,9 +32,9 @@
 
 def kernel(
     bands, slots,
-    waves_hbm, proj_hbm, miller_ref, lattice_ref, occupation_ref, species_ref, count_ref, coupling_ref,
+    waves_hbm, proj_hbm, miller_hbm, lattice_ref, occupation_ref, species_ref, count_ref, coupling_ref,
     forces_ref, stress_ref,
-    gath, waves, weights, spread, overlap, first_sum, second_sum, filling, part_ref,
+    gath, waves, weights, spread, overlap, first_sum, second_sum, filling, part_ref, miller_ref,
     local_sem, send_sem, recv_sem, pair_send, pair_recv, small_send, small_recv,
     first_send, first_recv, second_send, second_recv,
 ):
@@ -66,6 +66,8 @@
     own_copy.start()
     wave_copy = pltpu.make_async_copy(waves_hbm.at[:, pl.ds(begin, width)], waves.at[column], local_sem.at[1])
     wave_copy.start()
+    miller_copy = pltpu.make_async_copy(miller_hbm, miller_ref, local_sem.at[2])
+    miller_copy.start()
     barrier = pltpu.get_barrier_semaphore()
     for offset in range(1, peers):
         pl.semaphore_signal(barrier, inc=1, device_id=peer_id((rank + offset) % peers), device_id_type=MESH)
@@ -162,6 +164,7 @@
             part = gath.at[row, other, :, pl.ds(start, size)]
             pair_copy(part, part, piece).wait_recv()
             pass_on(row, other, piece)
+    miller_copy.wait()
     make_weights()
     part_ref[...] = jnp.zeros_like(part_ref)
 
@@ -302,10 +305,12 @@
             for index in range(pair):
                 waves[index, :, shared] = waves[index, :, shared] * keep
     for step in range(line):
-        if step and step == line - 1:
+        last = step > 0 and step == line - 1
+        if last:
+            each(step - 1, finish)
             take(step)
         each(step, project)
-        if step:
+        if step and not last:
             each(step - 1, finish)
     each(line - 1, finish)
 
@@ -385,7 +390,7 @@
     return pl.pallas_call(
         functools.partial(kernel, bands, slots),
         out_shape=(jax.ShapeDtypeStruct((3, 1), jnp.float32), jax.ShapeDtypeStruct((3, 3), jnp.float32)),
-        in_specs=[hbm, hbm, vmem, smem, vmem, smem, smem, vmem],
+        in_specs=[hbm, hbm, hbm, smem, vmem, smem, smem, vmem],
         out_specs=(vmem, vmem),
         scratch_shapes=[
             pltpu.VMEM((line, pair, 2 * PROJ, held), jnp.bfloat16),
@@ -397,7 +402,8 @@
             pltpu.VMEM((line, 8, LANES), jnp.float32),
             pltpu.VMEM((pair, 8, pair * 2 * band_count), jnp.float32),
             pltpu.VMEM((8, LANES), jnp.float32),
-            dma((2,)),
+            pltpu.VMEM((3, width), jnp.int32),
+            dma((3,)),
             dma((2, line, pair, PIECES)),
             dma((line, pair, PIECES)),
             dma((PIECES + 2,)),

time: 66.3 us -> 69.4 us (1.047)
  Pallas kernels: 63 us -> 66 us
    pallas_call x1, Pallas kernels: 63 us -> 66 us  [body(): pl.pallas_call(functools.partial(kernel, bands, slots), out_shape=(jax.Sh...]
where the time goes in v3:
time: 69.4 us; the launch traced here: 69.2 us
  Pallas kernels  66 us (95%)
  local copies, waits for them, and re-layouts  2.49 us (4%)
    pallas_call x1, Pallas kernels, body(): pl.pallas_call(functools.partial(kernel, bands, slots), out_shape=(jax.Sh...  66 us

profile of v3, /device:TPU:0, one launch (start us, length us, event | category | flops | bytes accessed | tf_op | source)
XLA Modules:
  0.0 69.2 jit_solution(5106891355815154483)
XLA Ops:
  0.6 66.0 %shard_map.95 = (f32[3,1]{1,0:T(4,128)}, f32[3,3]{1,0:T(4,128)}) custom-call(bf16[64,18816]{1,0:T(8,128)(2,1)} %bitcast.3, bf16[16,18816]{1,0:T(8,128)(2,1)} %bitcast.4, s32[3,18816]{1,0:T(4,128)} %miller_hbm.1, f32[3,3]{1,0:T(4,128)} %lattice_ref.1, f32[1,32]{1,0:T(1,128)} %bitcast.5, s32[8]{0:T(128)} %species_ref.1, s32[8]{0:T(128)} %count_ref.1, ...), custom_call_target="tpu_custom_call" | custom-call | tf_op jit(solution)/shard_map/pallas_call | solution.py:390
  66.7 1.3 %copy.10 = f32[3,1]{0,1:T(1,128)} copy(f32[3,1]{1,0:T(4,128)} %get-tuple-element.2) | data formatting | bytes 24 | tf_op jit(solution)/shard_map/pallas_call | solution.py:390
  68.0 1.2 %copy.12 = f32[3,3]{1,0:T(4,128)} copy(f32[3,3]{1,0:T(4,128)} %get-tuple-element.7) | data formatting | bytes 72
